TPU v7x, 32 devices: a whole 2x2x4 slice. The times are simulated.
32 devices in a mesh: row: 8 (over z, y), col: 4 (over x, core).
Axes of the slice: x: 2, y: 2, z: 4, core: 2. Of those that a mesh axis runs over, the one named last changes fastest.
Arguments:
- points: float32 [16, 4096], P(None, ('col', 'row')), may hold values from -5 to 5
- inv_scales: float32 [16], replicated, may hold values from 0.1 to 0.4
- amplitude: float32 [1], replicated, may hold values from 0.5 to 2
- noise_var: float32 [1], replicated, may hold values from 0.3 to 1
- targets: float32 [8, 4096], P(None, ('col', 'row')), may hold values from -6 to 6
- initial: float32 [8, 4096], P(None, ('col', 'row')), may hold values from -3 to 3
- ritz_basis: float32 [64, 4096], P(None, ('col', 'row')), may hold values from -0.09375 to 0.09375
Outputs:
- solution: float32 [8, 4096], P(None, ('col', 'row'))
- residual: float32 [8, 4096], P(None, ('col', 'row'))
All inputs are finite; a program needn't handle non-finite values.
Results may differ from a plain program's by a relative error of at most 0.00065.
Values sent between devices are 32-bit elements; how exact they have to be, the bound alone decides.
A program may use at most 128 MiB of HBM per device.

v0:
```python
import jax
import jax.numpy as jnp
from jax import lax
from jax.sharding import PartitionSpec as P

ITERS = 1
HIGH = lax.Precision.HIGHEST


def kernel_tile(col_x, col_sq, row_x, row_sq, gain):
    cross_term = jnp.dot(col_x.T, row_x, precision=HIGH, preferred_element_type=jnp.float32)
    distance = jnp.maximum(col_sq[:, None] + row_sq[None, :] - 2.0 * cross_term, 0.0)
    return gain * jnp.exp(-0.5 * distance)


def coarse_solve(factor, rhs_block):
    middle = lax.linalg.triangular_solve(factor, rhs_block, left_side=True, lower=True)
    return lax.linalg.triangular_solve(factor, middle, left_side=True, lower=True, transpose_a=True)


def matmul(left, right):
    return jnp.dot(left, right, precision=HIGH, preferred_element_type=jnp.float32)


def local(points, inv_scales, amplitude, noise_var, targets, initial, ritz_basis):
    gain = amplitude[0]
    nugget = noise_var[0]
    all_x = lax.all_gather(points, ("row", "col"), axis=1, tiled=True) * inv_scales[:, None]
    all_sq = jnp.sum(all_x * all_x, axis=0)
    row_x = points * inv_scales[:, None]
    row_sq = jnp.sum(row_x * row_x, axis=0)

    def apply_operator(vectors):
        partial_value = matmul(
            lax.all_gather(vectors, ("row", "col"), axis=1, tiled=True),
            kernel_tile(all_x, all_sq, row_x, row_sq, gain),
        )
        return partial_value + nugget * vectors

    rhs_count = initial.shape[0]
    applied_all = apply_operator(jnp.concatenate([initial, ritz_basis], 0))
    ritz_image = applied_all[rhs_count:]
    first_residual = targets - applied_all[:rhs_count]
    coarse, projected = lax.psum(
        (matmul(ritz_basis, ritz_image.T), matmul(ritz_basis, first_residual.T)), ("row", "col")
    )
    coarse = 0.5 * (coarse + coarse.T)
    factor = jnp.linalg.cholesky(coarse)
    coarse_inverse = coarse_solve(factor, jnp.eye(coarse.shape[0], dtype=jnp.float32))
    amounts = matmul(coarse_inverse, projected)
    solution = initial + matmul(amounts.T, ritz_basis)
    residual = first_residual - matmul(amounts.T, ritz_image)

    def residual_stats(current):
        return lax.psum(
            (matmul(ritz_image, current.T), jnp.sum(current * current, axis=1)), ("row", "col")
        )

    against, sq_norm = residual_stats(residual)
    direction = residual - matmul(matmul(coarse_inverse, against).T, ritz_basis)

    def plain_step(step, state):
        solution, residual, direction, sq_norm = state
        applied = apply_operator(direction)
        curvature = lax.psum(jnp.sum(direction * applied, axis=1), ("row", "col"))
        step_size = sq_norm / curvature
        solution = solution + step_size[:, None] * direction
        residual = residual - step_size[:, None] * applied
        against, new_norm = residual_stats(residual)
        correction = matmul(matmul(coarse_inverse, against).T, ritz_basis)
        direction = residual + (new_norm / sq_norm)[:, None] * direction - correction
        return (solution, residual, direction, new_norm)

    solution, residual, direction, sq_norm = lax.fori_loop(
        0, ITERS, plain_step, (solution, residual, direction, sq_norm)
    )
    return (solution, residual)


def solution(mesh):
    placed = (
        P(None, ("col", "row")),
        P(),
        P(),
        P(),
        P(None, ("col", "row")),
        P(None, ("col", "row")),
        P(None, ("col", "row")),
    )
    return jax.shard_map(
        local,
        mesh=mesh,
        in_specs=placed,
        out_specs=(P(None, ("col", "row")), P(None, ("col", "row"))),
        check_vma=False,
    )
```

profile of v0, /device:TPU:10, one launch (start us, length us, event | category | flops | bytes accessed | tf_op | source)
XLA Modules:
  0.0 250.7 jit_solution(7430495101600024024)
XLA Ops:
  7.2 0.7 constant_dynamic-update-slice_fusion.1
  7.9 0.8 constant_dynamic-update-slice_fusion
  8.7 0.6 copy-done.1
  10.6 0.8 multiply_reduce_fusion.1
  11.4 31.7 %all_gather.11 = f32[16,4096]{1,0:T(8,128)S(1)} all-gather(f32[16,128]{1,0:T(8,128)} %param.7), channel_id=1, replica_groups=mesh['row'=8,'col'=4] {'row','col'}, dimensions={1}, use_global_device_ids=true | all-gather | bytes 270336 | tf_op jit(solution)/shard_map/all_gather | solution.py:28
  43.1 0.8 multiply_reduce_fusion
  43.9 4.8 %fusion.4 = f32[4096,128]{1,0:T(8,128)S(1)} fusion(f32[128]{0:T(128)S(1)} %multiply_reduce_fusion.1, f32[4096]{0:T(1024)S(1)} %multiply_reduce_fusion, f32[]{:T(128)} %bitcast.38, f32[16,4096]{1,0:T(8,128)S(1)} %all_gather.11, f32[16]{0:T(128)} %param.8, f32[16,128]{1,0:T(8,128)} %param.7), kind=kOutput, calls=%fused_computation.5 | convolution fusion | flops 103876608 | bytes 2384452 | tf_op jit(solution)/shard_map/dot_general | solution.py:11
  48.7 16.1 %all-gather.2.cloned.1.call-done = f32[72,4096]{1,0:T(8,128)} async-done(((f32[72,128]{1,0:T(8,128)}), f32[72,4096]{1,0:T(8,128)}) %all-gather.2.cloned.1.call-update) | async-done | bytes 1179664 | tf_op jit(solution)/shard_map/all_gather | solution.py:35
  64.9 2.7 %convolution_add_fusion = f32[72,128]{1,0:T(8,128)S(1)} fusion(f32[72,4096]{1,0:T(8,128)} %all-gather.2.cloned.1.call-done, f32[4096,128]{1,0:T(8,128)S(1)} %fusion.4, f32[72,128]{1,0:T(8,128)S(1)} %copy-done.2, f32[]{:T(128)} %bitcast.39), kind=kOutput, calls=%fused_computation.6 | convolution fusion | flops 453003264 | bytes 3350532 | tf_op jit(solution)/shard_map/dot_general | solution.py:22
  67.6 0.2 convolution_bitcast_fusion
  68.0 40.1 %all-reduce.1 = (f32[64,64]{0,1:T(8,128)S(1)}, f32[64,8]{0,1:T(8,128)S(1)}) all-reduce(f32[64,64]{0,1:T(8,128)S(1)} %convolution_bitcast_fusion, f32[64,8]{0,1:T(8,128)S(1)} %convolution_bitcast_fusion.1), channel_id=1, replica_groups=mesh['row'=8,'col'=4] {'row','col'}, use_global_device_ids=true, to_apply=%region_2.0 | all-reduce | flops 4608 | bytes 36864 | tf_op jit(solution)/shard_map/psum | solution.py:44
  108.3 5.8 %cholesky.17 = f32[64,64]{1,0:T(8,128)S(1)} custom-call(f32[64,64]{1,0:T(8,128)S(1)} %fusion.13), custom_call_target="Cholesky" | custom-call | tf_op jit(solution)/shard_map/jit(cholesky)/cholesky | solution.py:48
  114.2 0.6 compare_reduce_fusion
  114.8 0.7 fusion.8
  115.5 4.9 %custom-call.8 = f32[1,64,64]{1,2,0:T(8,128)S(1)} custom-call(f32[1,64,64]{2,1,0:T(8,128)S(1)} %fusion.8), custom_call_target="InvertDiagBlocksLowerTriangular" | custom-call | tf_op jit(solution)/shard_map/triangular_solve | solution.py:18
  120.4 0.2 fusion.11
  120.9 0.3 multiply_reduce_fusion.3
  121.4 40.2 %psum.47 = f32[64,8]{1,0:T(8,128)S(1)} all-reduce(f32[64,8]{1,0:T(8,128)S(1)} %fusion.15), channel_id=1, replica_groups=mesh['row'=8,'col'=4] {'row','col'}, use_global_device_ids=true, to_apply=%region_8.0 | all-reduce | flops 512 | bytes 4096 | tf_op jit(solution)/shard_map/psum | solution.py:55
  161.8 0.2 convolution_subtract_fusion
  162.0 30.1 %all_gather.12 = f32[8,4096]{1,0:T(8,128)S(1)} all-gather(f32[8,128]{1,0:T(8,128)S(1)} %convolution_subtract_fusion), channel_id=1, replica_groups=mesh['row'=8,'col'=4] {'row','col'}, dimensions={1}, use_global_device_ids=true | all-gather | bytes 135168 | tf_op jit(solution)/shard_map/while/body/eval_jaxpr/all_gather | solution.py:35
  192.1 1.2 multiply_reduce_fusion.2
  193.3 49.1 %all-reduce = (f32[8]{0:T(128)S(1)}, f32[8]{0:T(128)S(1)}) all-reduce(f32[8]{0:T(128)S(1)} %get-tuple-element.34, f32[8]{0:T(128)S(1)} %get-tuple-element.36), channel_id=1, replica_groups=mesh['row'=8,'col'=4] {'row','col'}, use_global_device_ids=true, to_apply=%region_7.8 | all-reduce | flops 16 | bytes 128 | tf_op jit(solution)/shard_map/psum | solution.py:55
  242.4 0.7 fusion.5
  243.2 0.7 multiply_subtract_fusion
  (22 shorter events, 1.1 us)
Async XLA Ops:
  7.2 57.7 %all-gather.2.cloned.1.call-start = ((), (), s32[]{:S(2)}) async-start(), calls=%async_computation | async-start | bytes 1216512 | tf_op jit(solution)/shard_map/all_gather | solution.py:35
  8.7 0.6 copy-start.1
  10.6 54.3 %copy-start.2 = (f32[72,128]{1,0:T(8,128)S(1)}, f32[72,128]{1,0:T(8,128)}, u32[]{:S(2)}) copy-start(f32[72,128]{1,0:T(8,128)} %copy-done.1) | copy-start | bytes 110596
  48.7 18.9 %copy-start = (f32[64,128]{1,0:T(8,128)S(1)}, f32[64,128]{1,0:T(8,128)}, u32[]{:S(2)}) copy-start(f32[64,128]{1,0:T(8,128)} %param.13) | copy-start | bytes 98308
  48.7 19.1 %copy-start.3 = (f32[8,128]{1,0:T(8,128)S(1)}, f32[8,128]{1,0:T(8,128)}, u32[]{:S(2)}) copy-start(f32[8,128]{1,0:T(8,128)} %param.11) | copy-start | bytes 12292
  67.6 174.8 %copy-start.4 = (f32[8,128]{1,0:T(8,128)S(1)}, f32[8,128]{1,0:T(8,128)}, u32[]{:S(2)}) copy-start(f32[8,128]{1,0:T(8,128)} %param.12) | copy-start | bytes 12292
Sparse Core Ops, SparseCore 0:
  10.8 53.9 all-gather.1
where the time goes:
time: 251 us
  blocking collectives  191 us (76%)
  waiting for transfers between devices  16.1 us (6%)
  between operations  15.5 us (6%)
  other arithmetic  14.3 us (6%)
  matrix products  11.2 us (4%)
    psum x2, blocking collectives, residual_stats(): lax.psum((matmul(ritz_image, current.T), jnp.sum(current * current, axis=...  89.3 us
    psum x1, blocking collectives, local(): lax.psum((matmul(ritz_basis, ritz_image.T), matmul(ritz_basis, first_resi...  40.1 us
    all_gather x1, blocking collectives, local(): lax.all_gather(points, ('row', 'col'), axis=1, tiled=True)  31.7 us
    all_gather x1, blocking collectives, apply_operator(): lax.all_gather(vectors, ('row', 'col'), axis=1, tiled=True)  30.1 us
    all_gather x1, waiting for transfers between devices, apply_operator(): lax.all_gather(vectors, ('row', 'col'), axis=1, tiled=True)  16.1 us
    another operation x3, other arithmetic, local(): factor = jnp.linalg.cholesky(coarse)  6.52 us
    dot_general x10, matrix products, matmul(): jnp.dot(left, right, precision=HIGH, preferred_element_type=jnp.float32)  5.97 us
    another operation x2, other arithmetic, coarse_solve(): lax.linalg.triangular_solve(factor, middle, left_side=True, lower=True, t...  5.55 us
  transfers between devices with their start and end apart: 1, of which 1 were waited for; matrix products, arithmetic and copies ran while one was open for 3% of the time, Pallas kernels for 0%

commit v1 on v0

--- a/solution.py
+++ b/solution.py
@@ -42,7 +42,8 @@
     ritz_image = applied_all[rhs_count:]
     first_residual = targets - applied_all[:rhs_count]
     coarse, projected = lax.psum(
-        (matmul(ritz_basis, ritz_image.T), matmul(ritz_basis, first_residual.T)), ("row", "col")
+        lax.psum((matmul(ritz_basis, ritz_image.T), matmul(ritz_basis, first_residual.T)), "row"),
+        "col",
     )
     coarse = 0.5 * (coarse + coarse.T)
     factor = jnp.linalg.cholesky(coarse)

time: 251 us -> 256 us (1.020)
  blocking collectives: 191 us -> 196 us
    psum x0 -> x1, blocking collectives: none -> 10.6 us  [local(): lax.psum(lax.psum((matmul(ritz_basis, ritz_image.T), matmul(ritz_basis, f...]
    psum x1, blocking collectives: 40.1 us -> 33.1 us  [local(): lax.psum((matmul(ritz_basis, ritz_image.T), matmul(ritz_basis, first_resi...]
  transfers between devices with their start and end apart: 1 -> 1, of which waited for: 1 -> 1; matrix products, arithmetic and copies ran while one was open for 3% -> 2% of each run, Pallas kernels for 0% -> 0%
where the time goes in v1:
time: 256 us; the launch traced here: 255 us
  blocking collectives  196 us (77%)
  waiting for transfers between devices  16.1 us (6%)
  between operations  15.5 us (6%)
  other arithmetic  14.3 us (6%)
  matrix products  11.2 us (4%)
    psum x2, blocking collectives, residual_stats(): lax.psum((matmul(ritz_image, current.T), jnp.sum(current * current, axis=...  91.1 us
    psum x1, blocking collectives, local(): lax.psum((matmul(ritz_basis, ritz_image.T), matmul(ritz_basis, first_resi...  33.1 us
    all_gather x1, blocking collectives, local(): lax.all_gather(points, ('row', 'col'), axis=1, tiled=True)  31.7 us
    all_gather x1, blocking collectives, apply_operator(): lax.all_gather(vectors, ('row', 'col'), axis=1, tiled=True)  29.2 us
    all_gather x1, waiting for transfers between devices, apply_operator(): lax.all_gather(vectors, ('row', 'col'), axis=1, tiled=True)  16.1 us
    psum x1, blocking collectives, local(): lax.psum(lax.psum((matmul(ritz_basis, ritz_image.T), matmul(ritz_basis, f...  10.6 us
    another operation x3, other arithmetic, local(): factor = jnp.linalg.cholesky(coarse)  6.52 us
    dot_general x10, matrix products, matmul(): jnp.dot(left, right, precision=HIGH, preferred_element_type=jnp.float32)  5.97 us
  transfers between devices with their start and end apart: 1, of which 1 were waited for; matrix products, arithmetic and copies ran while one was open for 2% of the time, Pallas kernels for 0%

profile of v1, /device:TPU:10, one launch (start us, length us, event | category | flops | bytes accessed | tf_op | source)
XLA Modules:
  0.0 255.1 jit_solution(13083647837582029142)
XLA Ops:
  7.2 0.7 constant_dynamic-update-slice_fusion.1
  7.9 0.8 constant_dynamic-update-slice_fusion
  8.7 0.6 copy-done.1
  10.6 0.8 multiply_reduce_fusion.1
  11.4 31.7 %all_gather.11 = f32[16,4096]{1,0:T(8,128)S(1)} all-gather(f32[16,128]{1,0:T(8,128)} %param.7), channel_id=1, replica_groups=mesh['row'=8,'col'=4] {'row','col'}, dimensions={1}, use_global_device_ids=true | all-gather | bytes 270336 | tf_op jit(solution)/shard_map/all_gather | solution.py:28
  43.1 0.8 multiply_reduce_fusion
  43.9 4.8 %fusion.4 = f32[4096,128]{1,0:T(8,128)S(1)} fusion(f32[128]{0:T(128)S(1)} %multiply_reduce_fusion.1, f32[4096]{0:T(1024)S(1)} %multiply_reduce_fusion, f32[]{:T(128)} %bitcast.38, f32[16,4096]{1,0:T(8,128)S(1)} %all_gather.11, f32[16]{0:T(128)} %param.8, f32[16,128]{1,0:T(8,128)} %param.7), kind=kOutput, calls=%fused_computation.5 | convolution fusion | flops 103876608 | bytes 2384452 | tf_op jit(solution)/shard_map/dot_general | solution.py:11
  48.7 16.1 %all-gather.2.cloned.1.call-done = f32[72,4096]{1,0:T(8,128)} async-done(((f32[72,128]{1,0:T(8,128)}), f32[72,4096]{1,0:T(8,128)}) %all-gather.2.cloned.1.call-update) | async-done | bytes 1179664 | tf_op jit(solution)/shard_map/all_gather | solution.py:35
  64.9 2.7 %convolution_add_fusion = f32[72,128]{1,0:T(8,128)S(1)} fusion(f32[72,4096]{1,0:T(8,128)} %all-gather.2.cloned.1.call-done, f32[4096,128]{1,0:T(8,128)S(1)} %fusion.4, f32[72,128]{1,0:T(8,128)S(1)} %copy-done.2, f32[]{:T(128)} %bitcast.39), kind=kOutput, calls=%fused_computation.6 | convolution fusion | flops 453003264 | bytes 3350532 | tf_op jit(solution)/shard_map/dot_general | solution.py:22
  68.0 33.1 %all-reduce.1 = (f32[64,64]{0,1:T(8,128)S(1)}, f32[64,8]{0,1:T(8,128)S(1)}) all-reduce(f32[64,64]{0,1:T(8,128)S(1)} %convolution_bitcast_fusion, f32[64,8]{0,1:T(8,128)S(1)} %convolution_bitcast_fusion.1), channel_id=1, replica_groups=mesh['row'=8,'col'=4] {'row'}, use_global_device_ids=true, to_apply=%region_2.0 | all-reduce | flops 4608 | bytes 36864 | tf_op jit(solution)/shard_map/psum | solution.py:45
  101.1 10.6 %all-reduce.2 = (f32[64,64]{0,1:T(8,128)S(1)}, f32[64,8]{0,1:T(8,128)S(1)}) all-reduce(f32[64,64]{0,1:T(8,128)S(1)} %get-tuple-element.32, f32[64,8]{0,1:T(8,128)S(1)} %get-tuple-element.33), channel_id=1, replica_groups=mesh['row'=8,'col'=4] {'col'}, use_global_device_ids=true, to_apply=%region_3.0 | all-reduce | flops 4608 | bytes 36864 | tf_op jit(solution)/shard_map/psum | solution.py:44
  111.9 5.8 %cholesky.17 = f32[64,64]{1,0:T(8,128)S(1)} custom-call(f32[64,64]{1,0:T(8,128)S(1)} %fusion.13), custom_call_target="Cholesky" | custom-call | tf_op jit(solution)/shard_map/jit(cholesky)/cholesky | solution.py:49
  117.8 0.6 compare_reduce_fusion
  118.4 0.7 fusion.8
  119.1 4.9 %custom-call.8 = f32[1,64,64]{1,2,0:T(8,128)S(1)} custom-call(f32[1,64,64]{2,1,0:T(8,128)S(1)} %fusion.8), custom_call_target="InvertDiagBlocksLowerTriangular" | custom-call | tf_op jit(solution)/shard_map/triangular_solve | solution.py:18
  124.0 0.2 fusion.11
  124.5 0.3 multiply_reduce_fusion.3
  125.0 41.7 %psum.63 = f32[64,8]{1,0:T(8,128)S(1)} all-reduce(f32[64,8]{1,0:T(8,128)S(1)} %fusion.15), channel_id=1, replica_groups=mesh['row'=8,'col'=4] {'row','col'}, use_global_device_ids=true, to_apply=%region_10.0 | all-reduce | flops 512 | bytes 4096 | tf_op jit(solution)/shard_map/psum | solution.py:56
  166.8 0.2 convolution_subtract_fusion
  167.0 29.2 %all_gather.12 = f32[8,4096]{1,0:T(8,128)S(1)} all-gather(f32[8,128]{1,0:T(8,128)S(1)} %convolution_subtract_fusion), channel_id=1, replica_groups=mesh['row'=8,'col'=4] {'row','col'}, dimensions={1}, use_global_device_ids=true | all-gather | bytes 135168 | tf_op jit(solution)/shard_map/while/body/eval_jaxpr/all_gather | solution.py:35
  196.2 1.2 multiply_reduce_fusion.2
  197.4 49.4 %all-reduce = (f32[8]{0:T(128)S(1)}, f32[8]{0:T(128)S(1)}) all-reduce(f32[8]{0:T(128)S(1)} %get-tuple-element.36, f32[8]{0:T(128)S(1)} %get-tuple-element.38), channel_id=1, replica_groups=mesh['row'=8,'col'=4] {'row','col'}, use_global_device_ids=true, to_apply=%region_9.10 | all-reduce | flops 16 | bytes 128 | tf_op jit(solution)/shard_map/psum | solution.py:56
  246.8 0.7 fusion.5
  247.6 0.7 multiply_subtract_fusion
  (23 shorter events, 1.2 us)
Async XLA Ops:
  7.2 57.7 %all-gather.2.cloned.1.call-start = ((), (), s32[]{:S(2)}) async-start(), calls=%async_computation | async-start | bytes 1216512 | tf_op jit(solution)/shard_map/all_gather | solution.py:35
  8.7 0.6 copy-start.1
  10.6 54.3 %copy-start.2 = (f32[72,128]{1,0:T(8,128)S(1)}, f32[72,128]{1,0:T(8,128)}, u32[]{:S(2)}) copy-start(f32[72,128]{1,0:T(8,128)} %copy-done.1) | copy-start | bytes 110596
  48.7 18.9 %copy-start = (f32[64,128]{1,0:T(8,128)S(1)}, f32[64,128]{1,0:T(8,128)}, u32[]{:S(2)}) copy-start(f32[64,128]{1,0:T(8,128)} %param.13) | copy-start | bytes 98308
  48.7 19.1 %copy-start.3 = (f32[8,128]{1,0:T(8,128)S(1)}, f32[8,128]{1,0:T(8,128)}, u32[]{:S(2)}) copy-start(f32[8,128]{1,0:T(8,128)} %param.11) | copy-start | bytes 12292
  67.6 179.2 %copy-start.4 = (f32[8,128]{1,0:T(8,128)S(1)}, f32[8,128]{1,0:T(8,128)}, u32[]{:S(2)}) copy-start(f32[8,128]{1,0:T(8,128)} %param.12) | copy-start | bytes 12292
Sparse Core Ops, SparseCore 0:
  10.8 53.9 all-gather.1
